TPU v7x, 32 devices: a whole 2x2x4 slice. The times are simulated.
32 devices in a mesh: dp: 2 (over y), expert: 16 (over z, x, core).
Axes of the slice: x: 2, y: 2, z: 4, core: 2. Of those that a mesh axis runs over, the one named last changes fastest.
Arguments:
- tokens: bfloat16 [512, 4096], P(('dp', 'expert')), may hold values from -6 to 6
- routing: int32 [512, 2], P(('dp', 'expert')), may hold values from 0 to 7, as said below
- hidden_grad: bfloat16 [2048, 4096], P(('dp', 'expert')), may hold values from -3 to 3
- gate_weight: bfloat16 [4096, 65536], P(None, 'expert'), may hold values from -0.09375 to 0.09375
- up_weight: bfloat16 [4096, 65536], P(None, 'expert'), may hold values from -0.09375 to 0.09375
Outputs:
- token_grad: bfloat16 [512, 4096], P(('dp', 'expert'))
- gate_weight_grad: bfloat16 [4096, 65536], P('dp', 'expert')
- up_weight_grad: bfloat16 [4096, 65536], P('dp', 'expert')
Inputs may be any that keep to these rules, and one draw needn't show every extreme that they name: `routing`: the 2 entries of a token differ, and no device names one expert in more than 4 of its tokens.
All inputs are finite; a program needn't handle non-finite values.
Results may differ from a plain program's by a relative error of at most 0.0085.
Values may be sent and summed in bfloat16 or wider, within the bound.
A program may use at most 256 MiB of HBM per device.

v0:
```python
import functools

import jax
import jax.numpy as jnp
from jax import lax
from jax.experimental import pallas as pl
from jax.experimental.pallas import tpu as pltpu
from jax.sharding import PartitionSpec as P


EXPERTS = 8
CAP = 4
MIB = 1024 * 1024

BLOCK = 512
SLOTS = 6
TILE = 256
WEIGHT_BLOCK = 256
MESH = pl.DeviceIdType.MESH
TRANSPOSED = (((1,), (1,)), ((), ()))
LEADING = (((0,), (0,)), ((), ()))


def placement(routing, columns, expert_of, part_of, slot_of):
    count = routing.shape[0]
    column = lax.broadcasted_iota(jnp.int32, (count, columns), 1)
    expert, part, slot = expert_of(column), part_of(column), slot_of(column)
    first = jnp.where(routing[:, 0:1] == expert, 1.0, 0.0)
    second = jnp.where(routing[:, 1:2] == expert, 1.0, 0.0)
    earlier = jnp.where(
        lax.broadcasted_iota(jnp.int32, (count, count), 0)
        > lax.broadcasted_iota(jnp.int32, (count, count), 1),
        1.0,
        0.0,
    )
    before = jnp.dot(earlier, first + second, preferred_element_type=jnp.float32)
    slot = slot.astype(jnp.float32)
    placed = jnp.where(before == slot, first, 0.0) + jnp.where(before + first == slot, second, 0.0)
    return [jnp.where(part == h, placed, 0.0).astype(jnp.bfloat16) for h in range(2)]


def row_picker(rows, half):
    at = lax.broadcasted_iota(jnp.int32, (rows, 2 * rows), 0)
    column = lax.broadcasted_iota(jnp.int32, (rows, 2 * rows), 1)
    wanted = (at // CAP) * (2 * CAP) + at % CAP + half * CAP
    return jnp.where(column == wanted, 1.0, 0.0).astype(jnp.bfloat16)


def row_spreader(rows, half):
    column = lax.broadcasted_iota(jnp.int32, (2 * rows, rows), 1)
    at = lax.broadcasted_iota(jnp.int32, (2 * rows, rows), 0)
    wanted = (column // CAP) * (2 * CAP) + column % CAP + half * CAP
    return jnp.where(at == wanted, 1.0, 0.0).astype(jnp.bfloat16)


def hidden_kernel(
    dims,
    routing_ref, tokens_ref, hidden_hbm, gate_hbm, up_hbm,
    grads_hbm, half_ref, part_ref,
    out, parts, rows, hid, wts, total, grads,
    wts_sem, own_sem, grads_sem,
    hid_send, hid_recv, row_send, row_recv, side_send, side_recv,
    far_send, far_recv, last_send, last_recv,
):
    n_dp, n_expert, block, slots = dims
    replica, index = lax.axis_index("dp"), lax.axis_index("expert")
    shards = n_expert // EXPERTS
    peers = n_expert // 2
    chip, core = index // 2, index % 2
    sibling = chip * 2 + 1 - core
    other = 1 - replica
    count, width = rows.shape
    half = width // 2
    mine = width // n_dp
    steps = gate_hbm.shape[1] // block

    def weight_copies(step, slot):
        columns = pl.ds(pl.multiple_of(step * block, block), block)
        return (
            pltpu.make_async_copy(gate_hbm.at[:, columns], wts.at[slot, 0], wts_sem.at[slot, 0]),
            pltpu.make_async_copy(up_hbm.at[:, columns], wts.at[slot, 1], wts_sem.at[slot, 1]),
        )

    def own_copy(step):
        columns = pl.ds(pl.multiple_of(step * block, block), block)
        return pltpu.make_async_copy(hidden_hbm.at[:, columns], hid.at[step, replica], own_sem.at[step])

    def grads_copy(step):
        columns = pl.ds(pl.multiple_of(step * block, block), block)
        return pltpu.make_async_copy(grads.at[step], grads_hbm.at[:, :, columns], grads_sem.at[step])

    def peer(apart):
        return lax.rem(chip + apart + peers, peers) * 2 + core

    def place(replica_at, device):
        return replica_at * n_expert + device

    def hid_copy(step):
        return pltpu.make_async_remote_copy(
            hid.at[step, replica], hid.at[step, replica], hid_send.at[step], hid_recv.at[step],
            device_id=(other, index), device_id_type=MESH,
        )

    def hid_arrival(step):
        return pltpu.make_async_remote_copy(
            hid.at[step, other], hid.at[step, other], hid_send.at[step], hid_recv.at[step],
            device_id=(other, index), device_id_type=MESH,
        )

    def row_copy(apart):
        return pltpu.make_async_remote_copy(
            out.at[peer(apart) // shards], parts.at[place(replica, index)],
            row_send.at[apart], row_recv.at[apart],
            device_id=(replica, peer(apart)), device_id_type=MESH,
        )

    def moved(source, at, send, recv, apart, to):
        return pltpu.make_async_remote_copy(
            source, parts.at[at], send.at[apart], recv.at[apart], device_id=to, device_id_type=MESH
        )

    for step in range(steps):
        own_copy(step).start()
    for step in range(slots):
        for copy in weight_copies(step, step):
            copy.start()

    barrier = pltpu.get_barrier_semaphore()

    def greet(apart, carry):
        pl.semaphore_signal(barrier, inc=1, device_id=(replica, peer(apart)), device_id_type=MESH)
        return carry

    lax.fori_loop(1, peers, greet, 0)
    pl.semaphore_signal(barrier, inc=1, device_id=(replica, sibling), device_id_type=MESH)
    pl.semaphore_signal(barrier, inc=1, device_id=(other, index), device_id_type=MESH)

    picks = placement(
        routing_ref[...], EXPERTS * 2 * CAP,
        lambda j: j // (2 * CAP), lambda j: (j // CAP) % 2, lambda j: j % CAP,
    )
    sent = lax.dot_general(
        picks[0], tokens_ref[:, :half], LEADING, preferred_element_type=jnp.float32
    ) + lax.dot_general(picks[1], tokens_ref[:, half:], LEADING, preferred_element_type=jnp.float32)
    out[...] = sent.astype(jnp.bfloat16).reshape(out.shape)
    parts[place(replica, index)] = out[index // shards]
    total[...] = jnp.zeros_like(total)

    pl.semaphore_wait(barrier, peers + 1)

    def dispatch(apart, carry):
        row_copy(apart).start()
        return carry

    lax.fori_loop(1, peers, dispatch, 0)
    own_block = out.at[index // shards]
    own_at = place(replica, index)
    moved(own_block, own_at, side_send, side_recv, 0, (replica, sibling)).start()
    moved(own_block, own_at, far_send, far_recv, 0, (other, index)).start()
    early = min(2, steps)
    for step in range(early):
        own_copy(step).wait()
        hid_copy(step).start()

    def pass_on(apart, carry):
        at = place(replica, peer(-apart))
        moved(parts.at[at], at, row_send, row_recv, apart, (replica, sibling)).wait_recv()
        moved(parts.at[at], at, side_send, side_recv, apart, (replica, sibling)).start()
        moved(parts.at[at], at, far_send, far_recv, apart, (other, index)).start()
        return carry

    lax.fori_loop(1, peers, pass_on, 0)
    for step in range(early, steps):
        own_copy(step).wait()
        hid_copy(step).start()

    def share(apart, carry):
        at = place(other, peer(-apart))
        moved(parts.at[at], at, far_send, far_recv, apart, (other, index)).wait_recv()
        moved(parts.at[at], at, last_send, last_recv, apart, (replica, sibling)).start()
        return carry

    lax.fori_loop(0, peers, share, 0)

    def settle(apart, carry):
        their = lax.rem(chip - apart + peers, peers) * 2 + 1 - core
        at = place(replica, their)
        moved(parts.at[at], at, side_send, side_recv, apart, (replica, sibling)).wait_recv()
        at = place(other, their)
        moved(parts.at[at], at, last_send, last_recv, apart, (replica, sibling)).wait_recv()
        return carry

    lax.fori_loop(0, peers, settle, 0)

    group = min(count, 128)
    for h in range(2):
        pick = row_picker(group, h)
        for at in range(0, count, group):
            got = parts[pl.ds(at // CAP, group // CAP)].reshape(2 * group, half)
            rows[at : at + group, h * half : (h + 1) * half] = jnp.dot(
                pick, got, preferred_element_type=jnp.float32
            ).astype(jnp.bfloat16)

    def forward(slot, at):
        columns = pl.ds(at, TILE)
        gate_pre = jnp.dot(rows[...], wts[slot, 0, :, columns], preferred_element_type=jnp.float32)
        up_pre = jnp.dot(rows[...], wts[slot, 1, :, columns], preferred_element_type=jnp.float32)
        return gate_pre, up_pre

    def gradients(step, at, gate_pre, up_pre):
        grad_h = hid[step, :, :, at : at + TILE].reshape(count, TILE).astype(jnp.float32)
        sig = jax.nn.sigmoid(gate_pre)
        grads[step, 0, :, at : at + TILE] = (
            grad_h * up_pre * sig * (1.0 + gate_pre * (1.0 - sig))
        ).astype(jnp.bfloat16)
        grads[step, 1, :, at : at + TILE] = (grad_h * gate_pre * sig).astype(jnp.bfloat16)

    first_row = pl.multiple_of(replica * mine, mine)

    def backward(step, slot, at):
        features = pl.ds(first_row + at, TILE)
        total[:, at : at + TILE] += lax.dot_general(
            grads[step, 0], wts[slot, 0, features, :], TRANSPOSED, preferred_element_type=jnp.float32
        ) + lax.dot_general(
            grads[step, 1], wts[slot, 1, features, :], TRANSPOSED, preferred_element_type=jnp.float32
        )

    def ready(step, slot):
        for copy in weight_copies(step, slot):
            copy.wait()
        hid_arrival(step).wait_recv()

    ready(0, 0)
    for at in range(0, block, TILE):
        gradients(0, at, *forward(0, at))
    grads_copy(0).start()
    tiles = block // TILE
    share_of = mine // tiles

    def advance(step, carry):
        slot, before = lax.rem(step, slots), lax.rem(step - 1, slots)
        ready(step, slot)
        for tile in range(tiles):
            pre = forward(slot, tile * TILE)
            for at in range(tile * share_of, (tile + 1) * share_of, TILE):
                backward(step - 1, before, at)
            gradients(step, tile * TILE, *pre)
        grads_copy(step).start()

        @pl.when(step - 1 + slots < steps)
        def _():
            for copy in weight_copies(step - 1 + slots, before):
                copy.start()

        return carry

    lax.fori_loop(1, steps, advance, 0)
    for at in range(0, mine, TILE):
        backward(steps - 1, (steps - 1) % slots, at)

    half_ref[...] = rows[:, pl.ds(first_row, mine)]
    quarter = mine // 2
    for at in range(0, count, group):
        kept = total[at : at + group].astype(jnp.bfloat16)
        spread = jnp.dot(
            row_spreader(group, 0), kept[:, :quarter], preferred_element_type=jnp.float32
        ) + jnp.dot(row_spreader(group, 1), kept[:, quarter:], preferred_element_type=jnp.float32)
        part_ref[pl.ds(at // CAP, group // CAP)] = spread.astype(jnp.bfloat16).reshape(
            group // CAP, 2 * CAP, quarter
        )

    for step in range(steps):
        grads_copy(step).wait()
        hid_copy(step).wait_send()

    def finish(apart, carry):
        row_copy(apart).wait_send()
        return carry

    lax.fori_loop(1, peers, finish, 0)

    def finish_moved(apart, carry):
        at = place(replica, peer(-apart))
        moved(parts.at[at], at, side_send, side_recv, apart, (replica, sibling)).wait_send()
        moved(parts.at[at], at, far_send, far_recv, apart, (other, index)).wait_send()
        moved(parts.at[at], at, last_send, last_recv, apart, (replica, sibling)).wait_send()
        return carry

    lax.fori_loop(0, peers, finish_moved, 0)


def hidden_pass(routing, tokens, hidden, gate_weight, up_weight):
    n_dp, n_expert = lax.axis_size("dp"), lax.axis_size("expert")
    width = tokens.shape[1]
    span = gate_weight.shape[1]
    count = n_dp * hidden.shape[0]
    block = min(BLOCK, span)
    steps = span // block
    slots = min(SLOTS, steps)
    peers = n_expert // 2
    mine = width // n_dp
    vmem = pl.BlockSpec(memory_space=pltpu.VMEM)
    anywhere = pl.BlockSpec(memory_space=pl.ANY)
    blocks = n_dp * n_expert
    dma = pltpu.SemaphoreType.DMA
    return pl.pallas_call(
        functools.partial(hidden_kernel, (n_dp, n_expert, block, slots)),
        in_specs=[vmem, vmem, anywhere, anywhere, anywhere],
        out_specs=[anywhere, vmem, vmem],
        out_shape=[
            jax.ShapeDtypeStruct((2, count, span), jnp.bfloat16),
            jax.ShapeDtypeStruct((count, mine), jnp.bfloat16),
            jax.ShapeDtypeStruct((blocks, 2 * CAP, mine // 2), jnp.bfloat16),
        ],
        scratch_shapes=[
            pltpu.VMEM((EXPERTS, 2 * CAP, width // 2), jnp.bfloat16),
            pltpu.VMEM((blocks, 2 * CAP, width // 2), jnp.bfloat16),
            pltpu.VMEM((count, width), jnp.bfloat16),
            pltpu.VMEM((steps, n_dp, hidden.shape[0], block), jnp.bfloat16),
            pltpu.VMEM((slots, 2, width, block), jnp.bfloat16),
            pltpu.VMEM((count, mine), jnp.float32),
            pltpu.VMEM((steps, 2, count, block), jnp.bfloat16),
            dma((slots, 2)), dma((steps,)), dma((steps,)),
            dma((steps,)), dma((steps,)),
            dma((peers,)), dma((peers,)), dma((peers,)), dma((peers,)),
            dma((peers,)), dma((peers,)), dma((peers,)), dma((peers,)),
        ],
        cost_estimate=pl.CostEstimate(
            flops=6 * count * width * span,
            bytes_accessed=4 * width * span,
            transcendentals=count * span,
        ),
        compiler_params=pltpu.CompilerParams(
            collective_id=0, has_side_effects=True, vmem_limit_bytes=62 * MIB
        ),
    )(routing, tokens, hidden, gate_weight, up_weight)


def weight_kernel(half_ref, grads_ref, gate_ref, up_ref, turned_ref):
    @pl.when(pl.program_id(0) == 0)
    def _():
        turned_ref[...] = half_ref[...].T

    for at, out_ref in ((0, gate_ref), (1, up_ref)):
        out_ref[...] = jnp.dot(
            turned_ref[...], grads_ref[at], preferred_element_type=jnp.float32
        ).astype(out_ref.dtype)


def weight_pass(half, grads):
    count, mine = half.shape
    span = grads.shape[2]
    block = min(WEIGHT_BLOCK, span)
    result = jax.ShapeDtypeStruct((mine, span), jnp.bfloat16)
    out = pl.BlockSpec((mine, block), lambda j: (0, j))
    return pl.pallas_call(
        weight_kernel,
        grid=(span // block,),
        in_specs=[
            pl.BlockSpec((count, mine), lambda j: (0, 0)),
            pl.BlockSpec((2, count, block), lambda j: (0, 0, j)),
        ],
        out_specs=[out, out],
        out_shape=[result, result],
        scratch_shapes=[pltpu.VMEM((mine, count), jnp.bfloat16)],
        cost_estimate=pl.CostEstimate(
            flops=4 * count * mine * span, bytes_accessed=4 * mine * span, transcendentals=0
        ),
        compiler_params=pltpu.CompilerParams(
            dimension_semantics=("arbitrary",), vmem_limit_bytes=40 * MIB
        ),
    )(half, grads)


def return_kernel(shards, n_dp, routing_ref, back_ref, out_ref):
    blocks, deep, quarter = back_ref.shape
    sources = blocks // n_dp
    picks = placement(
        routing_ref[...], sources * deep,
        lambda j: j // (deep * shards), lambda j: (j // CAP) % 2, lambda j: j % CAP,
    )
    for replica in range(n_dp):
        got = back_ref[pl.ds(replica * sources, sources)].reshape(sources * deep, quarter)
        for h in range(2):
            at = (2 * replica + h) * quarter
            out_ref[:, at : at + quarter] = jnp.dot(
                picks[h], got, preferred_element_type=jnp.float32
            ).astype(out_ref.dtype)


def return_pass(routing, back, width):
    n_dp = lax.axis_size("dp")
    shards = lax.axis_size("expert") // EXPERTS
    vmem = pl.BlockSpec(memory_space=pltpu.VMEM)
    return pl.pallas_call(
        functools.partial(return_kernel, shards, n_dp),
        in_specs=[vmem, vmem],
        out_specs=vmem,
        out_shape=jax.ShapeDtypeStruct((routing.shape[0], width), jnp.bfloat16),
    )(routing, back)


def per_device(tokens, routing, hidden_grad, gate_weight, up_weight):
    grads, half, part = hidden_pass(routing, tokens, hidden_grad, gate_weight, up_weight)
    back = lax.all_to_all(part, ("dp", "expert"), split_axis=0, concat_axis=0, tiled=True)
    gate_weight_grad, up_weight_grad = weight_pass(half, grads)
    token_grad = return_pass(routing, back, tokens.shape[1])
    return token_grad, gate_weight_grad, up_weight_grad


def solution(mesh):
    in_specs = (
        P(("dp", "expert"), None),
        P(("dp", "expert"), None),
        P(("dp", "expert"), None),
        P(None, "expert"),
        P(None, "expert"),
    )
    out_specs = (P(("dp", "expert"), None), P("dp", "expert"), P("dp", "expert"))
    return jax.shard_map(
        per_device, mesh=mesh, in_specs=in_specs, out_specs=out_specs, check_vma=False
    )
```

profile of v0, /device:TPU:0, one launch (start us, length us, event | category | flops | bytes accessed | tf_op | source)
XLA Modules:
  0.0 74.6 jit_solution(5959085491210872734)
XLA Ops:
  0.6 1.3 %copy.9.routing_ref = s32[16,2]{1,0:T(8,128)} copy(s32[16,2]{0,1:T(2,128)} %param.6) | data formatting | bytes 256 | tf_op args[1]
  2.0 44.4 %shard_map.76 = (bf16[2,128,4096]{2,1,0:T(8,128)(2,1)}, bf16[128,2048]{1,0:T(8,128)(2,1)}, bf16[32,8,1024]{2,1,0:T(8,128)(2,1)}) custom-call(s32[16,2]{1,0:T(8,128)} %copy.9.routing_ref, bf16[16,4096]{1,0:T(8,128)(2,1)} %tokens_ref.1, bf16[64,4096]{1,0:T(8,128)(2,1)} %hidden_hbm.1, bf16[4096,4096]{1,0:T(8,128)(2,1)} %gate_hbm.1, bf16[4096,4096]{1,0:T(8,128)(2,1)} %up_hbm.1), custom_call_target="tpu_custom_call" | custom-call | flops 12884901888 | bytes 67108864 | tf_op jit(solution)/shard_map/pallas_call | solution.py:306
  46.4 5.7 %all-to-all-start = ((bf16[32,8,1024]{2,1,0:T(8,128)(2,1)}), bf16[32,8,1024]{2,1,0:T(8,128)(2,1)S(1)}, u32[]{:S(2)}, u32[]{:S(2)}) async-start(bf16[32,8,1024]{2,1,0:T(8,128)(2,1)} %get-tuple-element.8), calls=%async_computation | async-start | bytes 1048576 | tf_op jit(solution)/shard_map/all_to_all | solution.py:405
  52.1 0.0 copy-start
  52.1 1.6 %copy-done = bf16[2,128,4096]{2,1,0:T(8,128)(2,1)S(1)} copy-done((bf16[2,128,4096]{2,1,0:T(8,128)(2,1)S(1)}, bf16[2,128,4096]{2,1,0:T(8,128)(2,1)}, u32[]{:S(2)}) %copy-start) | copy-done | bytes 2097176
  53.7 0.0 copy-start.1
  53.7 1.0 %copy-done.1 = bf16[128,2048]{1,0:T(8,128)(2,1)S(1)} copy-done((bf16[128,2048]{1,0:T(8,128)(2,1)S(1)}, bf16[128,2048]{1,0:T(8,128)(2,1)}, u32[]{:S(2)}) %copy-start.1) | copy-done | bytes 524312
  54.8 16.9 %shard_map.78 = (bf16[2048,4096]{1,0:T(8,128)(2,1)}, bf16[2048,4096]{1,0:T(8,128)(2,1)}) custom-call(bf16[128,2048]{1,0:T(8,128)(2,1)S(1)} %copy-done.1, bf16[2,128,4096]{2,1,0:T(8,128)(2,1)S(1)} %copy-done), custom_call_target="tpu_custom_call" | custom-call | flops 4294967296 | bytes 33554432 | tf_op jit(solution)/shard_map/pallas_call | solution.py:356
  71.7 0.0 all-to-all-done.back_ref
  71.7 0.0 copy-start.2
  71.7 0.8 %copy-done.2 = bf16[32,8,1024]{2,1,0:T(8,128)(2,1)} copy-done((bf16[32,8,1024]{2,1,0:T(8,128)(2,1)}, bf16[32,8,1024]{2,1,0:T(8,128)(2,1)S(1)}, u32[]{:S(2)}) %copy-start.2) | copy-done | bytes 524312
  72.5 2.1 %shard_map.77 = bf16[16,4096]{1,0:T(8,128)(2,1)} custom-call(s32[16,2]{1,0:T(8,128)} %copy.9.routing_ref, bf16[32,8,1024]{2,1,0:T(8,128)(2,1)} %copy-done.2), custom_call_target="tpu_custom_call" | custom-call | tf_op jit(solution)/shard_map/pallas_call | solution.py:395
Async XLA Ops:
  46.4 25.2 %all-to-all-start = ((bf16[32,8,1024]{2,1,0:T(8,128)(2,1)}), bf16[32,8,1024]{2,1,0:T(8,128)(2,1)S(1)}, u32[]{:S(2)}, u32[]{:S(2)}) async-start(bf16[32,8,1024]{2,1,0:T(8,128)(2,1)} %get-tuple-element.8), calls=%async_computation | async-start | bytes 1048576 | tf_op jit(solution)/shard_map/all_to_all | solution.py:405
  52.1 1.6 %copy-start = (bf16[2,128,4096]{2,1,0:T(8,128)(2,1)S(1)}, bf16[2,128,4096]{2,1,0:T(8,128)(2,1)}, u32[]{:S(2)}) copy-start(bf16[2,128,4096]{2,1,0:T(8,128)(2,1)} %get-tuple-element.10.grads_ref) | copy-start | bytes 6291460
  53.7 1.0 %copy-start.1 = (bf16[128,2048]{1,0:T(8,128)(2,1)S(1)}, bf16[128,2048]{1,0:T(8,128)(2,1)}, u32[]{:S(2)}) copy-start(bf16[128,2048]{1,0:T(8,128)(2,1)} %get-tuple-element.9.half_ref) | copy-start | bytes 1572868
  71.7 0.8 %copy-start.2 = (bf16[32,8,1024]{2,1,0:T(8,128)(2,1)}, bf16[32,8,1024]{2,1,0:T(8,128)(2,1)S(1)}, u32[]{:S(2)}) copy-start(bf16[32,8,1024]{2,1,0:T(8,128)(2,1)S(1)} %all-to-all-done.back_ref) | copy-start | bytes 1572868
where the time goes:
time: 75 us; the launch traced here: 74.6 us
  Pallas kernels  63.5 us (85%)
  starting transfers between devices  5.68 us (8%)
  local copies, waits for them, and re-layouts  4.77 us (6%)
    pallas_call x1, Pallas kernels, hidden_pass(): pl.pallas_call(functools.partial(hidden_kernel, (n_dp, n_expert, block, s...  44.4 us
    pallas_call x1, Pallas kernels, weight_pass(): pl.pallas_call(weight_kernel, grid=(span // block,), in_specs=[pl.BlockSp...  16.9 us
    all_to_all x1, starting transfers between devices, per_device(): lax.all_to_all(part, ('dp', 'expert'), split_axis=0, concat_axis=0, tiled...  5.68 us
    unnamed x7, local copies, waits for them, and re-layouts  4.77 us
    pallas_call x1, Pallas kernels, return_pass(): pl.pallas_call(functools.partial(return_kernel, shards, n_dp), in_specs=[...  2.14 us
  transfers between devices with their start and end apart: 1, of which 0 were waited for; matrix products, arithmetic and copies ran while one was open for 0% of the time, Pallas kernels for 23%

commit v1 on v0

v1 whole, which is shorter than its diff:
```python
import functools

import jax
import jax.numpy as jnp
from jax import lax
from jax.experimental import pallas as pl
from jax.experimental.pallas import tpu as pltpu
from jax.sharding import PartitionSpec as P


EXPERTS = 8
CAP = 4
CAP_BITS = CAP.bit_length() - 1
MIB = 1024 * 1024
KERNEL_MIB = 63

TILE = 256
WIDE = 512
PIECES = 4
BANDS = 4
EARLY_BANDS = 1
ROW_BLOCK = 256
MESH = pl.DeviceIdType.MESH
TRANSPOSED = (((1,), (1,)), ((), ()))
LEADING = (((0,), (0,)), ((), ()))


def placement(routing, rows, expert_bits):
    count = routing.shape[1]
    row = lax.broadcasted_iota(jnp.int32, (rows, count), 0)
    expert, part = row >> expert_bits, (row >> CAP_BITS) & 1
    slot = (row & (CAP - 1)).astype(jnp.float32)
    first = jnp.where(routing[0:1] == expert, 1.0, 0.0)
    second = jnp.where(routing[1:2] == expert, 1.0, 0.0)
    earlier = jnp.where(
        lax.broadcasted_iota(jnp.int32, (count, count), 0)
        < lax.broadcasted_iota(jnp.int32, (count, count), 1),
        1.0,
        0.0,
    )
    before = jnp.dot(first + second, earlier, preferred_element_type=jnp.float32)
    placed = jnp.where(before == slot, first, 0.0) + jnp.where(before + first == slot, second, 0.0)
    return [jnp.where(part == h, placed, 0.0).astype(jnp.bfloat16) for h in range(2)]


def row_picker(rows, half):
    at = lax.broadcasted_iota(jnp.int32, (rows, 2 * rows), 0)
    column = lax.broadcasted_iota(jnp.int32, (rows, 2 * rows), 1)
    wanted = ((at >> CAP_BITS) << (CAP_BITS + 1)) + (at & (CAP - 1)) + half * CAP
    return jnp.where(column == wanted, 1.0, 0.0).astype(jnp.bfloat16)


def row_spreader(rows, half):
    column = lax.broadcasted_iota(jnp.int32, (2 * rows, rows), 1)
    at = lax.broadcasted_iota(jnp.int32, (2 * rows, rows), 0)
    wanted = ((column >> CAP_BITS) << (CAP_BITS + 1)) + (column & (CAP - 1)) + half * CAP
    return jnp.where(at == wanted, 1.0, 0.0).astype(jnp.bfloat16)


def hidden_kernel(
    dims,
    routing_hbm, tokens_hbm, hidden_hbm, gate_hbm, up_hbm,
    grads_hbm, turned_hbm, part_ref,
    routing_ref, tokens_ref, grads_ref, turned_ref, out, parts, rows, hid, near, ring, pre, kept,
    near_sem, ring_sem, own_sem, grads_sem, turned_sem, routing_sem, tokens_sem,
    hid_send, hid_recv, row_send, row_recv, side_send, side_recv,
    far_send, far_recv, last_send, last_recv,
):
    _, n_expert = dims
    replica, index = lax.axis_index("dp"), lax.axis_index("expert")
    shards = n_expert // EXPERTS
    peers = n_expert // 2
    chip, core = index // 2, index % 2
    sibling = chip * 2 + 1 - core
    other = 1 - replica
    _, count, mine = rows.shape
    half = parts.shape[3]
    span = gate_hbm.shape[1]
    piece = mine // PIECES
    tile = min(TILE, span)
    weights = (gate_hbm, up_hbm)

    def near_copy(at, which):
        source = pl.ds(pl.multiple_of(replica * mine + at * piece, piece), piece)
        return pltpu.make_async_copy(
            weights[which].at[source], near.at[which, pl.ds(at * piece, piece)], near_sem.at[at, which]
        )

    def ring_copy(at, which):
        source = pl.ds(pl.multiple_of(other * mine + at * piece, piece), piece)
        return pltpu.make_async_copy(
            weights[which].at[source], ring.at[at % 2, which], ring_sem.at[at, which]
        )

    own_copy = pltpu.make_async_copy(hidden_hbm, hid.at[replica], own_sem)
    routing_copy = pltpu.make_async_copy(routing_hbm, routing_ref, routing_sem)
    tokens_copy = pltpu.make_async_copy(tokens_hbm, tokens_ref, tokens_sem)
    grads_copy = pltpu.make_async_copy(grads_ref, grads_hbm, grads_sem)
    turned_copy = pltpu.make_async_copy(turned_ref, turned_hbm, turned_sem)

    def peer(apart):
        return lax.rem(chip + apart + peers, peers) * 2 + core

    def place(replica_at, device):
        return replica_at * n_expert + device

    def hid_copy(at, band):
        deep = hid.shape[1] // BANDS
        block = hid.at[at, pl.ds(band * deep, deep)]
        return pltpu.make_async_remote_copy(
            block, block, hid_send.at[band], hid_recv.at[band],
            device_id=(other, index), device_id_type=MESH,
        )

    def moved(source, at, part, send, recv, apart, to):
        return pltpu.make_async_remote_copy(
            source, parts.at[part, at], send.at[part, apart], recv.at[part, apart],
            device_id=to, device_id_type=MESH,
        )

    def passed(at, part, send, recv, apart, to):
        return moved(parts.at[part, at], at, part, send, recv, apart, to)

    barrier = pltpu.get_barrier_semaphore()

    def greet(apart, carry):
        pl.semaphore_signal(barrier, inc=1, device_id=(replica, peer(apart)), device_id_type=MESH)
        return carry

    lax.fori_loop(1, peers, greet, 0)
    pl.semaphore_signal(barrier, inc=1, device_id=(replica, sibling), device_id_type=MESH)
    pl.semaphore_signal(barrier, inc=1, device_id=(other, index), device_id_type=MESH)

    routing_copy.start()
    tokens_copy.start()
    own_copy.start()
    for at in range(2):
        for which in range(2):
            ring_copy(at, which).start(priority=1)
    for at in range(PIECES):
        for which in range(2):
            near_copy(at, which).start(priority=1)

    routing_copy.wait()
    tokens_copy.wait()
    picks = placement(routing_ref[...], EXPERTS * 2 * CAP, CAP_BITS + 1)
    for part in range(2):
        at = part * half
        sent = jnp.dot(
            picks[0], tokens_ref[:, at : at + half], preferred_element_type=jnp.float32
        ) + jnp.dot(
            picks[1], tokens_ref[:, mine + at : mine + at + half], preferred_element_type=jnp.float32
        )
        out[part] = sent.astype(jnp.bfloat16).reshape(EXPERTS, 2 * CAP, half)
        parts[part, place(replica, index)] = out[part, index // shards]

    pl.semaphore_wait(barrier, peers + 1)

    own_at = place(replica, index)
    for part in range(2):
        def dispatch(apart, carry):
            to = peer(apart)
            moved(
                out.at[part, to // shards], own_at, part, row_send, row_recv, apart, (replica, to)
            ).start()
            return carry

        lax.fori_loop(1, peers, dispatch, 0)
    for part in range(2):
        own_block = out.at[part, index // shards]
        moved(own_block, own_at, part, far_send, far_recv, 0, (other, index)).start()
        moved(own_block, own_at, part, side_send, side_recv, 0, (replica, sibling)).start()

    own_copy.wait()
    for band in range(EARLY_BANDS):
        hid_copy(replica, band).start()

    def pass_on(part):
        def step(apart, carry):
            at = place(replica, peer(-apart))
            passed(at, part, row_send, row_recv, apart, (replica, sibling)).wait_recv()
            passed(at, part, far_send, far_recv, apart, (other, index)).start()
            passed(at, part, side_send, side_recv, apart, (replica, sibling)).start()
            return carry

        lax.fori_loop(1, peers, step, 0)

    def share(part):
        def step(apart, carry):
            at = place(other, peer(-apart))
            passed(at, part, far_send, far_recv, apart, (other, index)).wait_recv()
            passed(at, part, last_send, last_recv, apart, (replica, sibling)).start()
            return carry

        lax.fori_loop(0, peers, step, 0)

    def settle(part):
        def step(apart, carry):
            their = lax.rem(chip - apart + peers, peers) * 2 + 1 - core
            passed(
                place(replica, their), part, side_send, side_recv, apart, (replica, sibling)
            ).wait_recv()
            passed(
                place(other, their), part, last_send, last_recv, apart, (replica, sibling)
            ).wait_recv()
            return carry

        lax.fori_loop(0, peers, step, 0)
        for side, h in ((0, replica), (1, other)):
            pick = row_picker(group, h)
            for at in range(0, count, group):
                got = parts[part, pl.ds(at // CAP, group // CAP)].reshape(2 * group, half)
                rows[side, at : at + group, part * half : (part + 1) * half] = jnp.dot(
                    pick, got, preferred_element_type=jnp.float32
                ).astype(jnp.bfloat16)

    group = min(count, 128)

    def ring_part(at, which, column):
        return jnp.dot(
            rows[1, :, at * piece : (at + 1) * piece],
            ring[at % 2, which, :, column : column + tile],
            preferred_element_type=jnp.float32,
        )

    pass_on(0)
    pass_on(1)
    for band in range(EARLY_BANDS, BANDS):
        hid_copy(replica, band).start()
    share(0)
    settle(0)
    for which in range(2):
        ring_copy(0, which).wait()
    for column in range(0, span, tile):
        for which in range(2):
            pre[which, :, column : column + tile] = ring_part(0, which, column)
    for which in range(2):
        ring_copy(2, which).start(priority=1)
    share(1)
    for which in range(2):
        ring_copy(1, which).wait()
    for column in range(0, span, tile):
        for which in range(2):
            pre[which, :, column : column + tile] += ring_part(1, which, column)
    for which in range(2):
        ring_copy(3, which).start(priority=1)
    settle(1)
    for at in range(PIECES):
        for which in range(2):
            near_copy(at, which).wait()
    for column in range(0, span, tile):
        for which in range(2):
            pre[which, :, column : column + tile] += jnp.dot(
                rows[0], near[which, :, column : column + tile], preferred_element_type=jnp.float32
            )
    turned_ref[...] = rows[0].T
    turned_copy.start()
    for at in range(2, PIECES):
        for which in range(2):
            ring_copy(at, which).wait()
    for band in range(BANDS):
        hid_copy(other, band).wait_recv()
    for column in range(0, span, tile):
        gate_pre, up_pre = (
            pre[which, :, column : column + tile]
            + ring_part(2, which, column)
            + ring_part(3, which, column)
            for which in range(2)
        )
        grad_h = hid[:, :, column : column + tile].reshape(count, tile).astype(jnp.float32)
        sig = jax.nn.sigmoid(gate_pre)
        grads_ref[0, :, column : column + tile] = (
            grad_h * up_pre * sig * (1.0 + gate_pre * (1.0 - sig))
        ).astype(jnp.bfloat16)
        grads_ref[1, :, column : column + tile] = (grad_h * gate_pre * sig).astype(jnp.bfloat16)

    grads_copy.start()
    for at in range(0, mine, WIDE):
        back = lax.dot_general(
            grads_ref[0], near[0, at : at + WIDE], TRANSPOSED, preferred_element_type=jnp.float32
        ) + lax.dot_general(
            grads_ref[1], near[1, at : at + WIDE], TRANSPOSED, preferred_element_type=jnp.float32
        )
        kept[:, at : at + WIDE] = back.astype(jnp.bfloat16)

    for at in range(0, count, group):
        spread = jnp.dot(
            row_spreader(group, 0), kept[at : at + group, :half], preferred_element_type=jnp.float32
        ) + jnp.dot(
            row_spreader(group, 1), kept[at : at + group, half:], preferred_element_type=jnp.float32
        )
        part_ref[pl.ds(at // CAP, group // CAP)] = spread.astype(jnp.bfloat16).reshape(
            group // CAP, 2 * CAP, half
        )

    for band in range(BANDS):
        hid_copy(replica, band).wait_send()
    grads_copy.wait()
    turned_copy.wait()
    for part in range(2):
        def finish(apart, carry):
            passed(own_at, part, row_send, row_recv, apart, (replica, sibling)).wait_send()
            return carry

        def finish_moved(apart, carry):
            at = place(replica, peer(-apart))
            passed(at, part, side_send, side_recv, apart, (replica, sibling)).wait_send()
            passed(at, part, far_send, far_recv, apart, (other, index)).wait_send()
            passed(at, part, last_send, last_recv, apart, (replica, sibling)).wait_send()
            return carry

        lax.fori_loop(1, peers, finish, 0)
        lax.fori_loop(0, peers, finish_moved, 0)


def hidden_pass(routing, tokens, hidden, gate_weight, up_weight):
    n_dp, n_expert = lax.axis_size("dp"), lax.axis_size("expert")
    width = tokens.shape[1]
    span = gate_weight.shape[1]
    own_rows = hidden.shape[0]
    count = n_dp * own_rows
    peers = n_expert // 2
    mine = width // n_dp
    half = mine // 2
    vmem = pl.BlockSpec(memory_space=pltpu.VMEM)
    anywhere = pl.BlockSpec(memory_space=pl.ANY)
    blocks = n_dp * n_expert
    dma = pltpu.SemaphoreType.DMA
    per_peer = dma((2, peers))
    return pl.pallas_call(
        functools.partial(hidden_kernel, (n_dp, n_expert)),
        in_specs=[anywhere] * 5,
        out_specs=[anywhere, anywhere, vmem],
        out_shape=[
            jax.ShapeDtypeStruct((2, count, span), jnp.bfloat16),
            jax.ShapeDtypeStruct((mine, count), jnp.bfloat16),
            jax.ShapeDtypeStruct((blocks, 2 * CAP, half), jnp.bfloat16),
        ],
        scratch_shapes=[
            pltpu.VMEM(routing.shape, routing.dtype),
            pltpu.VMEM(tokens.shape, tokens.dtype),
            pltpu.VMEM((2, count, span), jnp.bfloat16),
            pltpu.VMEM((mine, count), jnp.bfloat16),
            pltpu.VMEM((2, EXPERTS, 2 * CAP, half), jnp.bfloat16),
            pltpu.VMEM((2, blocks, 2 * CAP, half), jnp.bfloat16),
            pltpu.VMEM((2, count, mine), jnp.bfloat16),
            pltpu.VMEM((n_dp, own_rows, span), jnp.bfloat16),
            pltpu.VMEM((2, mine, span), jnp.bfloat16),
            pltpu.VMEM((2, 2, mine // PIECES, span), jnp.bfloat16),
            pltpu.VMEM((2, count, span), jnp.float32),
            pltpu.VMEM((count, mine), jnp.bfloat16),
            dma((PIECES, 2)), dma((PIECES, 2)), dma(()), dma(()), dma(()), dma(()), dma(()),
            dma((BANDS,)), dma((BANDS,)),
            per_peer, per_peer, per_peer, per_peer,
            per_peer, per_peer, per_peer, per_peer,
        ],
        cost_estimate=pl.CostEstimate(
            flops=6 * count * width * span,
            bytes_accessed=4 * width * span,
            transcendentals=count * span,
        ),
        compiler_params=pltpu.CompilerParams(
            collective_id=0, has_side_effects=True, vmem_limit_bytes=KERNEL_MIB * MIB
        ),
    )(routing, tokens, hidden, gate_weight, up_weight)


def weight_kernel(turned_ref, grads_ref, gate_ref, up_ref):
    for at, out_ref in ((0, gate_ref), (1, up_ref)):
        out_ref[...] = jnp.dot(
            turned_ref[...], grads_ref[at], preferred_element_type=jnp.float32
        ).astype(out_ref.dtype)


def weight_pass(turned, grads):
    mine, count = turned.shape
    span = grads.shape[2]
    block = min(ROW_BLOCK, mine)
    result = jax.ShapeDtypeStruct((mine, span), jnp.bfloat16)
    out = pl.BlockSpec((block, span), lambda j: (j, 0))
    return pl.pallas_call(
        weight_kernel,
        grid=(mine // block,),
        in_specs=[
            pl.BlockSpec((block, count), lambda j: (j, 0)),
            pl.BlockSpec((2, count, span), lambda j: (0, 0, 0)),
        ],
        out_specs=[out, out],
        out_shape=[result, result],
        cost_estimate=pl.CostEstimate(
            flops=4 * count * mine * span, bytes_accessed=4 * mine * span, transcendentals=0
        ),
        compiler_params=pltpu.CompilerParams(
            dimension_semantics=("arbitrary",), vmem_limit_bytes=KERNEL_MIB * MIB
        ),
    )(turned, grads)


def return_kernel(shards, n_dp, routing_ref, back_ref, out_ref):
    blocks, deep, quarter = back_ref.shape
    sources = blocks // n_dp
    picks = placement(routing_ref[...], sources * deep, (deep * shards).bit_length() - 1)
    for replica in range(n_dp):
        got = back_ref[pl.ds(replica * sources, sources)].reshape(sources * deep, quarter)
        for h in range(2):
            at = (2 * replica + h) * quarter
            out_ref[:, at : at + quarter] = lax.dot_general(
                picks[h], got, LEADING, preferred_element_type=jnp.float32
            ).astype(out_ref.dtype)


def return_pass(routing, back, width):
    n_dp = lax.axis_size("dp")
    shards = lax.axis_size("expert") // EXPERTS
    vmem = pl.BlockSpec(memory_space=pltpu.VMEM)
    return pl.pallas_call(
        functools.partial(return_kernel, shards, n_dp),
        in_specs=[vmem, vmem],
        out_specs=vmem,
        out_shape=jax.ShapeDtypeStruct((routing.shape[1], width), jnp.bfloat16),
        compiler_params=pltpu.CompilerParams(vmem_limit_bytes=16 * MIB),
    )(routing, back)


def per_device(tokens, routing, hidden_grad, gate_weight, up_weight):
    routing = routing.T
    grads, turned, part = hidden_pass(routing, tokens, hidden_grad, gate_weight, up_weight)
    back = lax.all_to_all(part, ("dp", "expert"), split_axis=0, concat_axis=0, tiled=True)
    gate_weight_grad, up_weight_grad = weight_pass(turned, grads)
    token_grad = return_pass(routing, back, tokens.shape[1])
    return token_grad, gate_weight_grad, up_weight_grad


def solution(mesh):
    in_specs = (
        P(("dp", "expert"), None),
        P(("dp", "expert"), None),
        P(("dp", "expert"), None),
        P(None, "expert"),
        P(None, "expert"),
    )
    out_specs = (P(("dp", "expert"), None), P("dp", "expert"), P("dp", "expert"))
    return jax.shard_map(
        per_device, mesh=mesh, in_specs=in_specs, out_specs=out_specs, check_vma=False
    )
```

time: 75 us -> 64.1 us (0.85)
  Pallas kernels: 63.5 us -> 57.2 us
  local copies, waits for them, and re-layouts: 4.77 us -> 0.01 us
  waiting for transfers between devices: 0.01 us -> 2.29 us
  starting transfers between devices: 5.68 us -> 3.75 us
    pallas_call x2, Pallas kernels: 61.4 us -> 56.1 us  [the longest x1 42.5 us: hidden_pass(): pl.pallas_call(functools.partial(hidden_kernel, (n_dp, n_expert)), in_spe...]
    unnamed x7 -> x2, local copies, waits for them, and re-layouts: 4.77 us -> 0.01 us
    all_to_all x1, waiting for transfers between devices: 0.01 us -> 2.29 us  [per_device(): lax.all_to_all(part, ('dp', 'expert'), split_axis=0, concat_axis=0, tiled...]
    all_to_all x1, starting transfers between devices: 5.68 us -> 3.75 us  [per_device(): lax.all_to_all(part, ('dp', 'expert'), split_axis=0, concat_axis=0, tiled...]
    pallas_call x1, Pallas kernels: 2.14 us -> 1.08 us  [return_pass(): pl.pallas_call(functools.partial(return_kernel, shards, n_dp), in_specs=[...]
  transfers between devices with their start and end apart: 1 -> 1, of which waited for: 0 -> 1; matrix products, arithmetic and copies ran while one was open for 0% -> 0% of each run, Pallas kernels for 23% -> 21%
where the time goes in v1:
time: 64.1 us; the launch traced here: 63.9 us
  Pallas kernels  57.2 us (89%)
  starting transfers between devices  3.75 us (6%)
  waiting for transfers between devices  2.29 us (4%)
  between operations  0.66 us (1%)
    pallas_call x1, Pallas kernels, hidden_pass(): pl.pallas_call(functools.partial(hidden_kernel, (n_dp, n_expert)), in_spe...  42.5 us
    pallas_call x1, Pallas kernels, weight_pass(): pl.pallas_call(weight_kernel, grid=(mine // block,), in_specs=[pl.BlockSp...  13.6 us
    all_to_all x1, starting transfers between devices, per_device(): lax.all_to_all(part, ('dp', 'expert'), split_axis=0, concat_axis=0, tiled...  3.75 us
    all_to_all x1, waiting for transfers between devices, per_device(): lax.all_to_all(part, ('dp', 'expert'), split_axis=0, concat_axis=0, tiled...  2.29 us
  transfers between devices with their start and end apart: 1, of which 1 were waited for; matrix products, arithmetic and copies ran while one was open for 0% of the time, Pallas kernels for 21%

profile of v1, /device:TPU:0, one launch (start us, length us, event | category | flops | bytes accessed | tf_op | source)
XLA Modules:
  0.0 63.9 jit_solution(5566973863929096020)
XLA Ops:
  0.6 42.5 %shard_map.76 = (bf16[2,128,4096]{2,1,0:T(8,128)(2,1)}, bf16[2048,128]{1,0:T(8,128)(2,1)}, bf16[32,8,1024]{2,1,0:T(8,128)(2,1)}) custom-call(s32[2,16]{1,0:T(2,128)} %bitcast.1, bf16[16,4096]{1,0:T(8,128)(2,1)} %tokens_hbm.1, bf16[64,4096]{1,0:T(8,128)(2,1)} %hidden_hbm.1, bf16[4096,4096]{1,0:T(8,128)(2,1)} %gate_hbm.1, bf16[4096,4096]{1,0:T(8,128)(2,1)} %up_hbm.1), custom_call_target="tpu_custom_call" | custom-call | flops 12884901888 | bytes 67108864 | tf_op jit(solution)/shard_map/pallas_call | solution.py:330
  43.1 0.0 copy-start
  43.1 3.8 %all-to-all-start = ((bf16[32,8,1024]{2,1,0:T(8,128)(2,1)}), bf16[32,8,1024]{2,1,0:T(8,128)(2,1)S(1)}, u32[]{:S(2)}, u32[]{:S(2)}) async-start(bf16[32,8,1024]{2,1,0:T(8,128)(2,1)} %get-tuple-element.8), calls=%async_computation | async-start | bytes 1048576 | tf_op jit(solution)/shard_map/all_to_all | solution.py:428
  46.9 13.6 %shard_map.78 = (bf16[2048,4096]{1,0:T(8,128)(2,1)}, bf16[2048,4096]{1,0:T(8,128)(2,1)}) custom-call(bf16[2048,128]{1,0:T(8,128)(2,1)} %get-tuple-element.9.turned_ref, bf16[2,128,4096]{2,1,0:T(8,128)(2,1)} %get-tuple-element.10.grads_ref), custom_call_target="tpu_custom_call" | custom-call | flops 4294967296 | bytes 33554432 | tf_op jit(solution)/shard_map/pallas_call | solution.py:381
  60.5 2.3 %all-to-all-done.back_ref = bf16[32,8,1024]{2,1,0:T(8,128)(2,1)S(1)} async-done(((bf16[32,8,1024]{2,1,0:T(8,128)(2,1)}), bf16[32,8,1024]{2,1,0:T(8,128)(2,1)S(1)}, u32[]{:S(2)}, u32[]{:S(2)}) %all-to-all-start) | async-done | bytes 524320 | tf_op jit(solution)/shard_map/all_to_all | solution.py:428
  62.8 0.0 copy-done
  62.8 1.1 %shard_map.77 = bf16[16,4096]{1,0:T(8,128)(2,1)} custom-call(s32[2,16]{1,0:T(2,128)S(1)} %bitcast.2, bf16[32,8,1024]{2,1,0:T(8,128)(2,1)S(1)} %all-to-all-done.back_ref), custom_call_target="tpu_custom_call" | custom-call | tf_op jit(solution)/shard_map/pallas_call | solution.py:416
Async XLA Ops:
  43.1 19.7 %copy-start = (s32[16,2]{0,1:T(2,128)S(1)}, s32[16,2]{0,1:T(2,128)}, u32[]{:S(2)}) copy-start(s32[16,2]{0,1:T(2,128)} %param.6) | copy-start | bytes 388
  43.1 19.6 %all-to-all-start = ((bf16[32,8,1024]{2,1,0:T(8,128)(2,1)}), bf16[32,8,1024]{2,1,0:T(8,128)(2,1)S(1)}, u32[]{:S(2)}, u32[]{:S(2)}) async-start(bf16[32,8,1024]{2,1,0:T(8,128)(2,1)} %get-tuple-element.8), calls=%async_computation | async-start | bytes 1048576 | tf_op jit(solution)/shard_map/all_to_all | solution.py:428

commit v2 on v1

--- a/solution.py
+++ b/solution.py
@@ -14,9 +14,9 @@
 MIB = 1024 * 1024
 KERNEL_MIB = 63
 
-TILE = 256
+TILE = 512
 WIDE = 512
-PIECES = 4
+GROUPS = 2
 BANDS = 4
 EARLY_BANDS = 1
 ROW_BLOCK = 256
@@ -61,7 +61,7 @@
     dims,
     routing_hbm, tokens_hbm, hidden_hbm, gate_hbm, up_hbm,
     grads_hbm, turned_hbm, part_ref,
-    routing_ref, tokens_ref, grads_ref, turned_ref, out, parts, rows, hid, near, ring, pre, kept,
+    routing_ref, tokens_ref, grads_ref, turned_ref, out, parts, rows, hid, near, ring, pre, total, kept,
     near_sem, ring_sem, own_sem, grads_sem, turned_sem, routing_sem, tokens_sem,
     hid_send, hid_recv, row_send, row_recv, side_send, side_recv,
     far_send, far_recv, last_send, last_recv,
@@ -76,21 +76,35 @@
     _, count, mine = rows.shape
     half = parts.shape[3]
     span = gate_hbm.shape[1]
-    piece = mine // PIECES
-    tile = min(TILE, span)
+    wide = span // GROUPS
+    tile = min(TILE, wide)
     weights = (gate_hbm, up_hbm)
 
-    def near_copy(at, which):
-        source = pl.ds(pl.multiple_of(replica * mine + at * piece, piece), piece)
+    def near_copy(group, part, which):
+        source = pl.ds(pl.multiple_of(replica * mine + part * half, half), half)
+        columns = pl.ds(group * wide, wide)
         return pltpu.make_async_copy(
-            weights[which].at[source], near.at[which, pl.ds(at * piece, piece)], near_sem.at[at, which]
-        )
-
-    def ring_copy(at, which):
-        source = pl.ds(pl.multiple_of(other * mine + at * piece, piece), piece)
+            weights[which].at[source, columns],
+            near.at[which, pl.ds(part * half, half), columns],
+            near_sem.at[group, part, which],
+        )
+
+    def ring_copy(group, part, which):
+        source = pl.ds(pl.multiple_of(other * mine + part * half, half), half)
         return pltpu.make_async_copy(
-            weights[which].at[source], ring.at[at % 2, which], ring_sem.at[at, which]
-        )
+            weights[which].at[source, pl.ds(group * wide, wide)],
+            ring.at[part, which],
+            ring_sem.at[group, part, which],
+        )
+
+    def loaded(group, part):
+        for which in range(2):
+            ring_copy(group, part, which).wait()
+            near_copy(group, part, which).wait()
+
+    def refill(part):
+        for which in range(2):
+            ring_copy(1, part, which).start(priority=1)
 
     own_copy = pltpu.make_async_copy(hidden_hbm, hid.at[replica], own_sem)
     routing_copy = pltpu.make_async_copy(routing_hbm, routing_ref, routing_sem)
@@ -105,8 +119,8 @@
         return replica_at * n_expert + device
 
     def hid_copy(at, band):
-        deep = hid.shape[1] // BANDS
-        block = hid.at[at, pl.ds(band * deep, deep)]
+        strip = span // BANDS
+        block = hid.at[at, :, pl.ds(band * strip, strip)]
         return pltpu.make_async_remote_copy(
             block, block, hid_send.at[band], hid_recv.at[band],
             device_id=(other, index), device_id_type=MESH,
@@ -134,12 +148,13 @@
     routing_copy.start()
     tokens_copy.start()
     own_copy.start()
-    for at in range(2):
+    for part in range(2):
         for which in range(2):
-            ring_copy(at, which).start(priority=1)
-    for at in range(PIECES):
+            ring_copy(0, part, which).start(priority=1)
+            near_copy(0, part, which).start(priority=1)
+    for part in range(2):
         for which in range(2):
-            near_copy(at, which).start(priority=1)
+            near_copy(1, part, which).start(priority=1)
 
     routing_copy.wait()
     tokens_copy.wait()
@@ -216,10 +231,36 @@
 
     group = min(count, 128)
 
-    def ring_part(at, which, column):
+    def product(part, which, column, start):
+        features = slice(part * half, (part + 1) * half)
         return jnp.dot(
-            rows[1, :, at * piece : (at + 1) * piece],
-            ring[at % 2, which, :, column : column + tile],
+            rows[0, :, features],
+            near[which, features, column : column + tile],
+            preferred_element_type=jnp.float32,
+        ) + jnp.dot(
+            rows[1, :, features],
+            ring[part, which, :, column - start : column - start + tile],
+            preferred_element_type=jnp.float32,
+        )
+
+    def gradients(column, gate_pre, up_pre):
+        grad_h = hid[:, :, column : column + tile].reshape(count, tile).astype(jnp.float32)
+        sig = jax.nn.sigmoid(gate_pre)
+        grads_ref[0, :, column : column + tile] = (
+            grad_h * up_pre * sig * (1.0 + gate_pre * (1.0 - sig))
+        ).astype(jnp.bfloat16)
+        grads_ref[1, :, column : column + tile] = (grad_h * gate_pre * sig).astype(jnp.bfloat16)
+
+    def arrived(bands):
+        for band in bands:
+            hid_copy(other, band).wait_recv()
+
+    def back(at, columns):
+        return lax.dot_general(
+            grads_ref[0, :, columns], near[0, at : at + WIDE, columns], TRANSPOSED,
+            preferred_element_type=jnp.float32,
+        ) + lax.dot_general(
+            grads_ref[1, :, columns], near[1, at : at + WIDE, columns], TRANSPOSED,
             preferred_element_type=jnp.float32,
         )
 
@@ -229,59 +270,38 @@
         hid_copy(replica, band).start()
     share(0)
     settle(0)
-    for which in range(2):
-        ring_copy(0, which).wait()
-    for column in range(0, span, tile):
+    loaded(0, 0)
+    for column in range(0, wide, tile):
         for which in range(2):
-            pre[which, :, column : column + tile] = ring_part(0, which, column)
-    for which in range(2):
-        ring_copy(2, which).start(priority=1)
+            pre[which, :, column : column + tile] = product(0, which, column, 0)
+    refill(0)
     share(1)
-    for which in range(2):
-        ring_copy(1, which).wait()
-    for column in range(0, span, tile):
-        for which in range(2):
-            pre[which, :, column : column + tile] += ring_part(1, which, column)
-    for which in range(2):
-        ring_copy(3, which).start(priority=1)
     settle(1)
-    for at in range(PIECES):
-        for which in range(2):
-            near_copy(at, which).wait()
-    for column in range(0, span, tile):
-        for which in range(2):
-            pre[which, :, column : column + tile] += jnp.dot(
-                rows[0], near[which, :, column : column + tile], preferred_element_type=jnp.float32
-            )
+    loaded(0, 1)
+    arrived(range(BANDS // 2))
+    for column in range(0, wide, tile):
+        gate_pre, up_pre = (
+            pre[which, :, column : column + tile] + product(1, which, column, 0) for which in range(2)
+        )
+        gradients(column, gate_pre, up_pre)
+    refill(1)
     turned_ref[...] = rows[0].T
     turned_copy.start()
-    for at in range(2, PIECES):
-        for which in range(2):
-            ring_copy(at, which).wait()
-    for band in range(BANDS):
-        hid_copy(other, band).wait_recv()
-    for column in range(0, span, tile):
+    columns = slice(0, wide)
+    for at in range(0, mine, WIDE):
+        total[:, at : at + WIDE] = back(at, columns)
+    loaded(1, 0)
+    loaded(1, 1)
+    arrived(range(BANDS // 2, BANDS))
+    for column in range(wide, span, tile):
         gate_pre, up_pre = (
-            pre[which, :, column : column + tile]
-            + ring_part(2, which, column)
-            + ring_part(3, which, column)
-            for which in range(2)
-        )
-        grad_h = hid[:, :, column : column + tile].reshape(count, tile).astype(jnp.float32)
-        sig = jax.nn.sigmoid(gate_pre)
-        grads_ref[0, :, column : column + tile] = (
-            grad_h * up_pre * sig * (1.0 + gate_pre * (1.0 - sig))
-        ).astype(jnp.bfloat16)
-        grads_ref[1, :, column : column + tile] = (grad_h * gate_pre * sig).astype(jnp.bfloat16)
-
+            product(0, which, column, wide) + product(1, which, column, wide) for which in range(2)
+        )
+        gradients(column, gate_pre, up_pre)
     grads_copy.start()
+    columns = slice(wide, span)
     for at in range(0, mine, WIDE):
-        back = lax.dot_general(
-            grads_ref[0], near[0, at : at + WIDE], TRANSPOSED, preferred_element_type=jnp.float32
-        ) + lax.dot_general(
-            grads_ref[1], near[1, at : at + WIDE], TRANSPOSED, preferred_element_type=jnp.float32
-        )
-        kept[:, at : at + WIDE] = back.astype(jnp.bfloat16)
+        kept[:, at : at + WIDE] = (total[:, at : at + WIDE] + back(at, columns)).astype(jnp.bfloat16)
 
     for at in range(0, count, group):
         spread = jnp.dot(
@@ -346,10 +366,11 @@
             pltpu.VMEM((2, count, mine), jnp.bfloat16),
             pltpu.VMEM((n_dp, own_rows, span), jnp.bfloat16),
             pltpu.VMEM((2, mine, span), jnp.bfloat16),
-            pltpu.VMEM((2, 2, mine // PIECES, span), jnp.bfloat16),
-            pltpu.VMEM((2, count, span), jnp.float32),
+            pltpu.VMEM((2, 2, half, span // GROUPS), jnp.bfloat16),
+            pltpu.VMEM((2, count, span // GROUPS), jnp.float32),
+            pltpu.VMEM((count, mine), jnp.float32),
             pltpu.VMEM((count, mine), jnp.bfloat16),
-            dma((PIECES, 2)), dma((PIECES, 2)), dma(()), dma(()), dma(()), dma(()), dma(()),
+            dma((GROUPS, 2, 2)), dma((GROUPS, 2, 2)), dma(()), dma(()), dma(()), dma(()), dma(()),
             dma((BANDS,)), dma((BANDS,)),
             per_peer, per_peer, per_peer, per_peer,
             per_peer, per_peer, per_peer, per_peer,

time: 64.1 us -> 63.2 us (0.986)
  Pallas kernels: 57.2 us -> 56.1 us
    pallas_call x1, Pallas kernels: 42.5 us -> 41.4 us  [hidden_pass(): pl.pallas_call(functools.partial(hidden_kernel, (n_dp, n_expert)), in_spe...]
  transfers between devices with their start and end apart: 1 -> 1, of which waited for: 1 -> 1; matrix products, arithmetic and copies ran while one was open for 0% -> 0% of each run, Pallas kernels for 21% -> 22%
where the time goes in v2:
time: 63.2 us; the launch traced here: 63 us
  Pallas kernels  56.1 us (89%)
  starting transfers between devices  3.95 us (6%)
  waiting for transfers between devices  2.29 us (4%)
  between operations  0.66 us (1%)
    pallas_call x1, Pallas kernels, hidden_pass(): pl.pallas_call(functools.partial(hidden_kernel, (n_dp, n_expert)), in_spe...  41.4 us
    pallas_call x1, Pallas kernels, weight_pass(): pl.pallas_call(weight_kernel, grid=(mine // block,), in_specs=[pl.BlockSp...  13.6 us
    all_to_all x1, starting transfers between devices, per_device(): lax.all_to_all(part, ('dp', 'expert'), split_axis=0, concat_axis=0, tiled...  3.95 us
    all_to_all x1, waiting for transfers between devices, per_device(): lax.all_to_all(part, ('dp', 'expert'), split_axis=0, concat_axis=0, tiled...  2.29 us
  transfers between devices with their start and end apart: 1, of which 1 were waited for; matrix products, arithmetic and copies ran while one was open for 0% of the time, Pallas kernels for 22%

profile of v2, /device:TPU:0, one launch (start us, length us, event | category | flops | bytes accessed | tf_op | source)
XLA Modules:
  0.0 63.0 jit_solution(11683042130686048579)
XLA Ops:
  0.6 41.4 %shard_map.76 = (bf16[2,128,4096]{2,1,0:T(8,128)(2,1)}, bf16[2048,128]{1,0:T(8,128)(2,1)}, bf16[32,8,1024]{2,1,0:T(8,128)(2,1)}) custom-call(s32[2,16]{1,0:T(2,128)} %bitcast.1, bf16[16,4096]{1,0:T(8,128)(2,1)} %tokens_hbm.1, bf16[64,4096]{1,0:T(8,128)(2,1)} %hidden_hbm.1, bf16[4096,4096]{1,0:T(8,128)(2,1)} %gate_hbm.1, bf16[4096,4096]{1,0:T(8,128)(2,1)} %up_hbm.1), custom_call_target="tpu_custom_call" | custom-call | flops 12884901888 | bytes 67108864 | tf_op jit(solution)/shard_map/pallas_call | solution.py:350
  42.0 0.0 copy-start
  42.1 3.9 %all-to-all-start = ((bf16[32,8,1024]{2,1,0:T(8,128)(2,1)}), bf16[32,8,1024]{2,1,0:T(8,128)(2,1)S(1)}, u32[]{:S(2)}, u32[]{:S(2)}) async-start(bf16[32,8,1024]{2,1,0:T(8,128)(2,1)} %get-tuple-element.8), calls=%async_computation | async-start | bytes 1048576 | tf_op jit(solution)/shard_map/all_to_all | solution.py:449
  46.0 13.6 %shard_map.78 = (bf16[2048,4096]{1,0:T(8,128)(2,1)}, bf16[2048,4096]{1,0:T(8,128)(2,1)}) custom-call(bf16[2048,128]{1,0:T(8,128)(2,1)} %get-tuple-element.9.turned_ref, bf16[2,128,4096]{2,1,0:T(8,128)(2,1)} %get-tuple-element.10.grads_ref), custom_call_target="tpu_custom_call" | custom-call | flops 4294967296 | bytes 33554432 | tf_op jit(solution)/shard_map/pallas_call | solution.py:402
  59.6 2.3 %all-to-all-done.back_ref = bf16[32,8,1024]{2,1,0:T(8,128)(2,1)S(1)} async-done(((bf16[32,8,1024]{2,1,0:T(8,128)(2,1)}), bf16[32,8,1024]{2,1,0:T(8,128)(2,1)S(1)}, u32[]{:S(2)}, u32[]{:S(2)}) %all-to-all-start) | async-done | bytes 524320 | tf_op jit(solution)/shard_map/all_to_all | solution.py:449
  61.9 0.0 copy-done
  61.9 1.1 %shard_map.77 = bf16[16,4096]{1,0:T(8,128)(2,1)} custom-call(s32[2,16]{1,0:T(2,128)S(1)} %bitcast.2, bf16[32,8,1024]{2,1,0:T(8,128)(2,1)S(1)} %all-to-all-done.back_ref), custom_call_target="tpu_custom_call" | custom-call | tf_op jit(solution)/shard_map/pallas_call | solution.py:437
Async XLA Ops:
  42.0 19.9 %copy-start = (s32[16,2]{0,1:T(2,128)S(1)}, s32[16,2]{0,1:T(2,128)}, u32[]{:S(2)}) copy-start(s32[16,2]{0,1:T(2,128)} %param.6) | copy-start | bytes 388
  42.1 19.8 %all-to-all-start = ((bf16[32,8,1024]{2,1,0:T(8,128)(2,1)}), bf16[32,8,1024]{2,1,0:T(8,128)(2,1)S(1)}, u32[]{:S(2)}, u32[]{:S(2)}) async-start(bf16[32,8,1024]{2,1,0:T(8,128)(2,1)} %get-tuple-element.8), calls=%async_computation | async-start | bytes 1048576 | tf_op jit(solution)/shard_map/all_to_all | solution.py:449
